TPU v7x, 512 devices: a whole 4x4x16 slice. The times are simulated.
512 devices in a mesh: sp: 64 (over z_lo, x, core), dp: 8 (over y, z_hi).
Axes of the slice: x: 4, y: 4, z: 16 (z_hi: 2, z_lo: 8; z = z_hi * 8 + z_lo), core: 2. Of those that a mesh axis runs over, the one named last changes fastest.
Arguments:
- queries: bfloat16 [24576, 24, 128], P(('dp', 'sp')), parts along dimension 0, may hold values from -12 to 12
- keys: bfloat16 [24576, 24, 128], P(('dp', 'sp')), parts along dimension 0, may hold values from -6 to 6
- values: bfloat16 [24576, 24, 128], P(('dp', 'sp')), parts along dimension 0, may hold values from -6 to 6
Outputs:
- attended: bfloat16 [24576, 3072], P(('dp', 'sp')), parts along dimension 0
There are 8 independent parts, one for each index of `dp`. A program takes and returns all parts, laid end to end along the dimension named above; each array names one. Nothing has to cross between parts.
All inputs are finite; a program needn't handle non-finite values.
Results may differ from a plain program's by a relative error of at most 0.0049.
Values may be sent and summed in bfloat16 or wider, within the bound.
A program may use at most 64 MiB of HBM per device.

v0:
```python
import jax
import jax.numpy as jnp
from jax import lax
from jax.sharding import Mesh
from jax.sharding import PartitionSpec as P

HGROUPS = 8
SP = ("sp_0", "sp_1", "sp_2")
DP_SP = ("dp", "sp_0", "sp_1", "sp_2")


def in_one_piece(arrays, axis, split_dim, concat_dim, along):
    ends, at = ([], 0)
    for a in arrays[:-1]:
        at += a.shape[along]
        ends.append(at)
    both = jnp.concatenate(arrays, axis=along)
    return tuple(
        jnp.split(
            lax.all_to_all(both, axis, split_axis=split_dim, concat_axis=concat_dim, tiled=True),
            ends,
            axis=along,
        )
    )


def split_up(shard, dim, peers):
    dims = shard.shape
    parts = shard.reshape(*dims[:dim], peers, dims[dim] // peers, *dims[dim + 1 :])
    return jnp.moveaxis(parts, dim, 0)


def laid_out(parts, dim):
    parts = jnp.moveaxis(parts, 0, dim)
    dims = parts.shape
    return parts.reshape(*dims[:dim], dims[dim] * dims[dim + 1], *dims[dim + 2 :])


def turned_blocks(parts, axes, sequence):
    dims = [lax.axis_size(a) for a in axes]
    parts = parts.reshape(*dims, *parts.shape[1:])
    for k in sequence:
        parts = lax.all_to_all(parts, axes[k], split_axis=k, concat_axis=k, tiled=True)
    return parts.reshape(-1, *parts.shape[len(axes) :])


def core_and_chips(shard, groups, sequence, split_dim, concat_dim):
    peers = lax.axis_size(groups[0]) * lax.axis_size(groups[1])
    parts = split_up(shard, split_dim, peers)
    return laid_out(turned_blocks(parts, groups, sequence), concat_dim)


def attend(triple):
    head_q, head_k, head_v = triple
    scale = 1.0 / head_q.shape[-1] ** 0.5
    scores = jnp.dot(head_q, head_k.T, preferred_element_type=jnp.float32) * scale
    weights = jax.nn.softmax(scores, axis=-1).astype(jnp.bfloat16)
    return jnp.dot(weights, head_v, preferred_element_type=jnp.float32)


def to_owners(field, groups, blocks):
    tokens = field.shape[0]
    feat = field.shape[1] * field.shape[2] // groups
    shaped = field.reshape(blocks, tokens // blocks, groups, feat)
    shaped = shaped.transpose(2, 0, 1, 3)
    return shaped.reshape(groups * blocks, tokens // blocks, feat)


def to_copies(field, groups, blocks):
    tokens = field.shape[0]
    feat = field.shape[1] * field.shape[2] // groups
    shaped = field.reshape(tokens, groups, feat).transpose(1, 0, 2)
    copies = jnp.broadcast_to(shaped[:, None], (groups, blocks, tokens, feat))
    return copies.reshape(groups * blocks, tokens, feat)


def from_owners(received, groups, blocks):
    rows = received.shape[1]
    feat = received.shape[2]
    shaped = received.reshape(groups, blocks, rows, feat).transpose(1, 2, 0, 3)
    return shaped.reshape(blocks * rows, groups * feat)


def shards(queries, keys, values):
    tokens, heads, width = queries.shape
    groups = HGROUPS
    blocks = lax.axis_size(SP) // groups
    per_group = heads // groups
    send_q = to_owners(queries, groups, blocks)
    send_k = to_copies(keys, groups, blocks)
    send_v = to_copies(values, groups, blocks)
    got_q, got_k, got_v = in_one_piece((send_q, send_k, send_v), SP, 0, 0, 1)
    local_q = got_q.reshape(-1, per_group, width).transpose(1, 0, 2)
    local_k = got_k.reshape(-1, per_group, width).transpose(1, 0, 2)
    local_v = got_v.reshape(-1, per_group, width).transpose(1, 0, 2)
    result = lax.map(attend, (local_q, local_k, local_v))
    count = result.shape[1]
    local_out = result.transpose(1, 0, 2).reshape(count, per_group * width).astype(jnp.bfloat16)
    outgoing = local_out.reshape(groups * blocks, tokens // blocks, per_group * width)
    returned = core_and_chips(outgoing, (("sp_0", "sp_1"), "sp_2"), (1, 0), 0, 0)
    return from_owners(returned, groups, blocks)


def solution(mesh):
    finer = Mesh(mesh.devices.reshape(8, 4, 2, mesh.shape["dp"]), ("sp_0", "sp_1", "sp_2", "dp"))
    return jax.shard_map(
        shards,
        mesh=finer,
        in_specs=(P(DP_SP, None, None), P(DP_SP, None, None), P(DP_SP, None, None)),
        out_specs=P(DP_SP, None),
        check_vma=False,
    )
```

profile of v0, /device:TPU:24, one launch (start us, length us, event | category | flops | bytes accessed | tf_op | source)
XLA Modules:
  0.0 321.1 jit_solution(11848974450281129456)
XLA Ops:
  0.0 1.1 reshape.46
  1.1 0.1 copy.38
  1.2 0.2 copy.27
  1.4 1.1 reshape.48
  2.5 1.1 reshape.50
  3.7 0.2 broadcast_in_dim.11
  3.9 0.2 broadcast_in_dim.10
  4.1 4.0 %pad_maximum_fusion = bf16[64,102,384]{2,1,0:T(8,128)(2,1)} fusion(bf16[64,48,384]{2,1,0:T(8,128)(2,1)S(1)} %bitcast.47, bf16[64,48,384]{2,1,0:T(8,128)(2,1)S(1)} %bitcast.48, bf16[64,6,384]{2,1,0:T(8,128)(2,1)S(1)} %copy.27), kind=kLoop, calls=%fused_computation.15 | loop fusion | flops 15040512 | bytes 10027008 | tf_op jit(solution)/shard_map/concatenate | solution.py:17
  8.1 16.2 %all-to-all-start = ((bf16[64,102,384]{2,1,0:T(8,128)(2,1)}), bf16[64,102,384]{2,1,0:T(8,128)(2,1)}, u32[]{:S(2)}, u32[]{:S(2)}) async-start(bf16[64,102,384]{2,1,0:T(8,128)(2,1)} %pad_maximum_fusion), calls=%async_computation | async-start | bytes 10223616 | tf_op jit(solution)/shard_map/all_to_all | solution.py:20
  24.3 225.5 %all-to-all-done = bf16[64,102,384]{2,1,0:T(8,128)(2,1)} async-done(((bf16[64,102,384]{2,1,0:T(8,128)(2,1)}), bf16[64,102,384]{2,1,0:T(8,128)(2,1)}, u32[]{:S(2)}, u32[]{:S(2)}) %all-to-all-start) | async-done | bytes 5013536 | tf_op jit(solution)/shard_map/all_to_all | solution.py:20
  249.9 1.0 split.12
  250.9 0.2 reshape.52
  251.1 7.7 %fusion.13 = (bf16[64,48,384]{2,1,0:T(8,128)(2,1)}, bf16[64,48,384]{2,1,0:T(8,128)(2,1)}) fusion(bf16[64,102,384]{2,1,0:T(8,128)(2,1)} %all-to-all-done), kind=kLoop, calls=%fused_computation.19 | loop fusion | bytes 9437184 | tf_op jit(solution)/shard_map/split | solution.py:19
  258.8 5.9 %reshape.54 = bf16[3072,3,128]{2,1,0:T(4,128)(2,1)S(1)} reshape(bf16[64,48,384]{2,1,0:T(8,128)(2,1)} %get-tuple-element.60) | data formatting | bytes 4718592 | tf_op jit(solution)/shard_map/reshape | solution.py:95
  264.7 1.8 copy.30
  266.5 0.0 copy-start
  266.5 7.1 %reshape.53 = bf16[3072,3,128]{2,1,0:T(4,128)(2,1)} reshape(bf16[64,48,384]{2,1,0:T(8,128)(2,1)} %get-tuple-element.61) | data formatting | bytes 4718592 | tf_op jit(solution)/shard_map/reshape | solution.py:94
  273.6 2.2 copy.29
  275.8 0.0 copy-done
  275.8 11.4 %while.10 = (s32[]{:T(128)}, bf16[3,384,128]{2,1,0:T(8,128)(2,1)S(1)}, bf16[3,384,128]{2,1,0:T(8,128)(2,1)S(1)}, bf16[3,3072,128]{2,1,0:T(8,128)(2,1)S(1)}, bf16[3,3072,128]{2,1,0:T(8,128)(2,1)}, /*index=5*/s32[]{:T(128)}) while((s32[]{:T(128)}, bf16[3,384,128]{2,1,0:T(8,128)(2,1)S(1)}, bf16[3,384,128]{2,1,0:T(8,128)(2,1)S(1)}, ...), condition=%wide.region_3.4_spmd, body=%wide.region_0.3_spmd.sunk | while | flops 612236544 | bytes 16034381 | solution.py:96
  275.9 0.9 fusion.19
  276.7 0.8 fusion.20
  277.5 2.1 fusion.21
  279.6 0.9 fusion.19
  280.5 0.8 fusion.20
  281.3 2.1 fusion.21
  283.4 0.9 fusion.19
  284.3 0.8 fusion.20
  285.1 2.1 fusion.21
  287.2 0.3 copy.31
  287.5 0.3 convert_element_type.21
  287.8 0.1 copy.32
  287.8 4.0 %all_to_all.15 = bf16[32,2,1,6,384]{4,0,3,2,1:T(8,128)(2,1)S(1)} all-to-all(bf16[32,2,1,6,384]{4,0,3,2,1:T(8,128)(2,1)S(1)} %copy.32), channel_id=1, replica_groups=mesh['sp_0'=8,'sp_1'=4,'sp_2'=2,'dp'=8] {'sp_2'}, dimensions={1} | all-to-all | bytes 589824 | tf_op jit(solution)/shard_map/all_to_all | solution.py:43
  291.8 0.3 copy.33
  292.1 27.9 %all_to_all.16 = bf16[32,2,1,6,384]{4,1,3,2,0:T(2,128)(2,1)S(1)} all-to-all(bf16[32,2,1,6,384]{4,1,3,2,0:T(2,128)(2,1)S(1)} %copy.33), channel_id=1, replica_groups=mesh['sp_0'=8,'sp_1'=4,'sp_2'=2,'dp'=8] {'sp_0','sp_1'}, dimensions={0} | all-to-all | bytes 589824 | tf_op jit(solution)/shard_map/all_to_all | solution.py:43
  320.0 0.2 copy.34
  320.2 0.1 reshape_reshape_reshape.4
  320.4 0.8 copy.36
  (5 shorter events, 0.2 us)
Async XLA Ops:
  8.1 241.8 %all-to-all-start = ((bf16[64,102,384]{2,1,0:T(8,128)(2,1)}), bf16[64,102,384]{2,1,0:T(8,128)(2,1)}, u32[]{:S(2)}, u32[]{:S(2)}) async-start(bf16[64,102,384]{2,1,0:T(8,128)(2,1)} %pad_maximum_fusion), calls=%async_computation | async-start | bytes 10223616 | tf_op jit(solution)/shard_map/all_to_all | solution.py:20
  266.5 9.3 %copy-start = (bf16[3,384,128]{2,1,0:T(8,128)(2,1)S(1)}, bf16[3,384,128]{2,1,0:T(8,128)(2,1)}, u32[]{:S(2)}) copy-start(bf16[3,384,128]{2,1,0:T(8,128)(2,1)} %custom-call) | copy-start | bytes 884740
where the time goes:
time: 322 us; the launch traced here: 321 us
  waiting for transfers between devices  226 us (70%)
  local copies, waits for them, and re-layouts  32 us (10%)
  blocking collectives  31.9 us (10%)
  starting transfers between devices  16.2 us (5%)
  matrix products  8.97 us (3%)
  other arithmetic  6.34 us (2%)
    all_to_all x1, waiting for transfers between devices, in_one_piece(): lax.all_to_all(both, axis, split_axis=split_dim, concat_axis=concat_dim,...  226 us
    all_to_all x2, blocking collectives, turned_blocks(): lax.all_to_all(parts, axes[k], split_axis=k, concat_axis=k, tiled=True)  31.9 us
    all_to_all x1, starting transfers between devices, in_one_piece(): lax.all_to_all(both, axis, split_axis=split_dim, concat_axis=concat_dim,...  16.2 us
    split x2, local copies, waits for them, and re-layouts, in_one_piece(): jnp.split(lax.all_to_all(both, axis, split_axis=split_dim, concat_axis=co...  8.75 us
    reshape x1, local copies, waits for them, and re-layouts, shards(): local_k = got_k.reshape(-1, per_group, width).transpose(1, 0, 2)  7.08 us
  transfers between devices with their start and end apart: 1, of which 1 were waited for; matrix products, arithmetic and copies ran while one was open for 0% of the time, Pallas kernels for 0%

commit v1 on v0

v1 whole, which is shorter than its diff:
```python
import functools
import math

import jax
import jax.numpy as jnp
from jax import lax
from jax.experimental import pallas as pl
from jax.experimental.pallas import tpu as pltpu
from jax.sharding import Mesh
from jax.sharding import PartitionSpec as P

NZ, NX = 8, 4
CHIPS = NZ * NX
HEADS, WIDTH = 24, 128
FIRST = 1
ROWS = HEADS // NX
MESH_IDS = pl.DeviceIdType.MESH


def chip(index):
    return {"sp_0": lax.div(index, NX), "sp_1": lax.rem(index, NX)}


def kernel(q_hbm, k_hbm, v_hbm, out_ref, raw, wide, stage, recv, far, outs,
           load_sem, send_sem, recv_sem, swap_send, swap_recv, back_send, back_recv):
    tokens = raw.shape[1]
    z, x, core = lax.axis_index("sp_0"), lax.axis_index("sp_1"), lax.axis_index("sp_2")
    me = z * NX + x
    head = (z - FIRST) * NX + x
    is_owner = (z >= FIRST) & (z < FIRST + ROWS)

    loads = [
        pltpu.make_async_copy(hbm, raw.at[t], load_sem.at[t])
        for t, hbm in enumerate((q_hbm, k_hbm, v_hbm))
    ]
    for load in loads:
        load.start()

    barrier = pltpu.get_barrier_semaphore()

    @pl.loop(1, CHIPS)
    def _(i):
        pl.semaphore_signal(barrier, inc=1, device_id=chip(lax.rem(me + i, CHIPS)), device_id_type=MESH_IDS)

    pl.semaphore_signal(barrier, inc=1, device_id={"sp_2": 1 - core}, device_id_type=MESH_IDS)

    for t in range(3):
        loads[t].wait()
        wide[t] = raw[t].astype(jnp.float32).reshape(tokens * HEADS, WIDTH)
        for h in range(HEADS):
            stage[h, t] = wide[t, pl.ds(h, tokens, stride=HEADS), :].astype(jnp.bfloat16)

    pl.semaphore_wait(barrier, CHIPS)

    def to_owner(i):
        row = lax.div(i, NX)
        row = jnp.where(z >= NZ // 2, row, ROWS - 1 - row)
        h = row * NX + lax.rem(x + 1 + i, NX)
        copy = pltpu.make_async_remote_copy(
            src_ref=stage.at[h], dst_ref=recv.at[me], send_sem=send_sem.at[h], recv_sem=recv_sem.at[me],
            device_id=chip(FIRST * NX + h), device_id_type=MESH_IDS,
        )
        return h, copy

    @pl.loop(0, HEADS)
    def _(i):
        h, copy = to_owner(i)

        @pl.when(FIRST * NX + h != me)
        def _():
            copy.start()

    def back(peer):
        return pltpu.make_async_remote_copy(
            src_ref=outs.at[peer],
            dst_ref=out_ref.at[:, pl.ds(pl.multiple_of(head * WIDTH, WIDTH), WIDTH)],
            send_sem=back_send.at[peer], recv_sem=back_recv.at[head],
            device_id=chip(peer), device_id_type=MESH_IDS,
        )

    def swap(row):
        chunk = pl.ds(row * NX, NX)
        return pltpu.make_async_remote_copy(
            src_ref=recv.at[chunk, pl.ds(1, 2)], dst_ref=far.at[chunk],
            send_sem=swap_send.at[row], recv_sem=swap_recv.at[row],
            device_id={"sp_2": 1 - core}, device_id_type=MESH_IDS,
        )

    @pl.when(is_owner)
    def _():
        recv[me] = stage[head]

        @pl.loop(0, NZ)
        def _(row):
            @pl.loop(0, NX)
            def _(j):
                source = row * NX + j

                @pl.when(source != me)
                def _():
                    pltpu.make_async_copy(recv.at[source], recv.at[source], recv_sem.at[source]).wait()

            swap(row).start()

        @pl.loop(0, NZ)
        def _(row):
            swap(row).wait_recv()

        factor = math.log2(math.e) / WIDTH**0.5
        dims = (((1,), (1,)), ((), ()))

        @pl.loop(0, NZ)
        def _(row):
            q = recv[pl.ds(row * NX, NX), 0].reshape(NX * tokens, WIDTH)
            k_near = recv[:, 1].reshape(CHIPS * tokens, WIDTH)
            k_far = far[:, 0].reshape(CHIPS * tokens, WIDTH)
            s_near = lax.dot_general(q, k_near, dims, preferred_element_type=jnp.float32)
            s_far = lax.dot_general(q, k_far, dims, preferred_element_type=jnp.float32)
            top = jnp.maximum(
                jnp.max(s_near, axis=1, keepdims=True), jnp.max(s_far, axis=1, keepdims=True)
            )
            p_near = jnp.exp2((s_near - top) * factor)
            p_far = jnp.exp2((s_far - top) * factor)
            total = jnp.sum(p_near, axis=1, keepdims=True) + jnp.sum(p_far, axis=1, keepdims=True)
            v_near = recv[:, 2].reshape(CHIPS * tokens, WIDTH)
            v_far = far[:, 1].reshape(CHIPS * tokens, WIDTH)
            acc = jnp.dot(p_near.astype(jnp.bfloat16), v_near, preferred_element_type=jnp.float32)
            acc += jnp.dot(p_far.astype(jnp.bfloat16), v_far, preferred_element_type=jnp.float32)
            result = (acc / total).astype(jnp.bfloat16)
            outs[pl.ds(row * NX, NX)] = result.reshape(NX, tokens, WIDTH)

            @pl.loop(0, NX)
            def _(j):
                peer = row * NX + j

                @pl.when(peer != me)
                def _():
                    back(peer).start()

                @pl.when(peer == me)
                def _():
                    out_ref[:, pl.ds(pl.multiple_of(head * WIDTH, WIDTH), WIDTH)] = outs[peer]

        @pl.loop(0, NZ)
        def _(row):
            swap(row).wait_send()

        @pl.loop(0, CHIPS)
        def _(peer):
            @pl.when(peer != me)
            def _():
                back(peer).wait_send()

    @pl.loop(0, HEADS)
    def _(h):
        @pl.when(FIRST * NX + h != me)
        def _():
            pltpu.make_async_copy(stage.at[h], stage.at[h], send_sem.at[h]).wait()
            pltpu.make_async_copy(outs.at[0], outs.at[0], back_recv.at[h]).wait()


def shards(queries, keys, values):
    tokens = queries.shape[0]
    dma = pltpu.SemaphoreType.DMA
    block = (tokens, WIDTH)
    return pl.pallas_call(
        kernel,
        out_shape=jax.ShapeDtypeStruct((tokens, HEADS * WIDTH), jnp.bfloat16),
        in_specs=[pl.BlockSpec(memory_space=pl.ANY)] * 3,
        out_specs=pl.BlockSpec(memory_space=pltpu.VMEM),
        scratch_shapes=[
            pltpu.VMEM((3, tokens, HEADS, WIDTH), jnp.bfloat16),
            pltpu.VMEM((3, tokens * HEADS, WIDTH), jnp.float32),
            pltpu.VMEM((HEADS, 3, *block), jnp.bfloat16),
            pltpu.VMEM((CHIPS, 3, *block), jnp.bfloat16),
            pltpu.VMEM((CHIPS, 2, *block), jnp.bfloat16),
            pltpu.VMEM((CHIPS, *block), jnp.bfloat16),
            dma((3,)),
            dma((HEADS,)),
            dma((CHIPS,)),
            dma((NZ,)),
            dma((NZ,)),
            dma((CHIPS,)),
            dma((HEADS,)),
        ],
        compiler_params=pltpu.CompilerParams(
            collective_id=0, has_side_effects=True, vmem_limit_bytes=48 * 1024 * 1024
        ),
    )(queries, keys, values)


def solution(mesh):
    finer = Mesh(mesh.devices.reshape(NZ, NX, 2, mesh.shape["dp"]), ("sp_0", "sp_1", "sp_2", "dp"))
    tokens = P(("dp", "sp_0", "sp_1", "sp_2"), None, None)
    return jax.shard_map(
        shards,
        mesh=finer,
        in_specs=(tokens,) * 3,
        out_specs=P(("dp", "sp_0", "sp_1", "sp_2"), None),
        check_vma=False,
    )
```

time: 322 us -> 76.5 us (0.24)
  the two profiles are of different devices: /device:TPU:24 before, /device:TPU:504 now
where the time goes in v1:
time: 76.5 us; the launch traced here: 75.7 us
  Pallas kernels  72.1 us (94%)
  local copies, waits for them, and re-layouts  3.6 us (5%)
    pallas_call x1, Pallas kernels, shards(): pl.pallas_call(kernel, out_shape=jax.ShapeDtypeStruct((tokens, HEADS * WI...  72.1 us
    unnamed x7, local copies, waits for them, and re-layouts  3.6 us

profile of v1, /device:TPU:504, one launch (start us, length us, event | category | flops | bytes accessed | tf_op | source)
XLA Modules:
  0.0 75.7 jit_solution(13967011270442083213)
XLA Ops:
  0.0 0.0 copy-start
  0.0 1.0 %copy-done = bf16[48,24,128]{2,1,0:T(8,128)(2,1)S(1)} copy-done((bf16[48,24,128]{2,1,0:T(8,128)(2,1)S(1)}, bf16[48,24,128]{2,1,0:T(8,128)(2,1)}, u32[]{:S(2)}) %copy-start) | copy-done | bytes 294936
  1.0 0.0 copy-start.1
  1.0 1.0 %copy-done.1 = bf16[48,24,128]{2,1,0:T(8,128)(2,1)S(1)} copy-done((bf16[48,24,128]{2,1,0:T(8,128)(2,1)S(1)}, bf16[48,24,128]{2,1,0:T(8,128)(2,1)}, u32[]{:S(2)}) %copy-start.1) | copy-done | bytes 294936
  1.9 0.0 copy-start.2
  1.9 1.0 %copy-done.2 = bf16[48,24,128]{2,1,0:T(8,128)(2,1)S(1)} copy-done((bf16[48,24,128]{2,1,0:T(8,128)(2,1)S(1)}, bf16[48,24,128]{2,1,0:T(8,128)(2,1)}, u32[]{:S(2)}) %copy-start.2) | copy-done | bytes 294936
  2.9 72.1 %shard_map.37 = bf16[48,3072]{1,0:T(8,128)(2,1)S(1)} custom-call(bf16[48,24,128]{2,1,0:T(8,128)(2,1)S(1)} %copy-done, bf16[48,24,128]{2,1,0:T(8,128)(2,1)S(1)} %copy-done.1, bf16[48,24,128]{2,1,0:T(8,128)(2,1)S(1)} %copy-done.2), custom_call_target="tpu_custom_call" | custom-call | tf_op jit(solution)/shard_map/pallas_call | solution.py:166
  75.0 0.7 copy.5
Async XLA Ops:
  0.0 1.0 %copy-start = (bf16[48,24,128]{2,1,0:T(8,128)(2,1)S(1)}, bf16[48,24,128]{2,1,0:T(8,128)(2,1)}, u32[]{:S(2)}) copy-start(bf16[48,24,128]{2,1,0:T(8,128)(2,1)} %q_hbm.1) | copy-start | bytes 884740
  1.0 1.0 %copy-start.1 = (bf16[48,24,128]{2,1,0:T(8,128)(2,1)S(1)}, bf16[48,24,128]{2,1,0:T(8,128)(2,1)}, u32[]{:S(2)}) copy-start(bf16[48,24,128]{2,1,0:T(8,128)(2,1)} %k_hbm.1) | copy-start | bytes 884740
  1.9 1.0 %copy-start.2 = (bf16[48,24,128]{2,1,0:T(8,128)(2,1)S(1)}, bf16[48,24,128]{2,1,0:T(8,128)(2,1)}, u32[]{:S(2)}) copy-start(bf16[48,24,128]{2,1,0:T(8,128)(2,1)} %v_hbm.1) | copy-start | bytes 884740

commit v2 on v1

v2 whole, which is shorter than its diff:
```python
import math

import jax
import jax.numpy as jnp
from jax import lax
from jax.experimental import pallas as pl
from jax.experimental.pallas import tpu as pltpu
from jax.sharding import Mesh
from jax.sharding import PartitionSpec as P

NZ, NX = 8, 4
CHIPS = NZ * NX
HEADS, WIDTH = 24, 128
FIRST = 1
ROWS = HEADS // NX
SKIP = FIRST * NX
MESH_IDS = pl.DeviceIdType.MESH


def kernel(q_hbm, k_hbm, v_hbm, out_ref, raw, wide, stage, stage_q, near, queries, far, outs,
           load_sem, kv_send, kv_recv, q_send, q_recv, swap_send, swap_recv, back_send, back_recv, ready):
    tokens = raw.shape[1]
    z, x, core = lax.axis_index("sp_0"), lax.axis_index("sp_1"), lax.axis_index("sp_2")
    me = z * NX + x
    head = me - SKIP
    is_owner = (z >= FIRST) & (z < FIRST + ROWS)

    loads = [
        pltpu.make_async_copy(hbm, raw.at[t], load_sem.at[t])
        for t, hbm in enumerate((k_hbm, v_hbm, q_hbm))
    ]
    for load in loads:
        load.start()

    barrier = pltpu.get_barrier_semaphore()

    def signal(semaphore, where):
        pl.semaphore_signal(semaphore, inc=1, device_id=where, device_id_type=MESH_IDS)

    def columns_of(body):
        for step in range(NX):
            to = x + step
            body(jnp.where(to >= NX, to - NX, to))

    @pl.when(is_owner)
    def _():
        signal(barrier, {"sp_2": 1 - core})

        @pl.loop(x + 1, NX)
        def _(to):
            signal(barrier, {"sp_1": to})

        @pl.loop(z + 1, NZ)
        def _(row):
            columns_of(lambda to: signal(barrier, {"sp_0": row, "sp_1": to}))

        columns_of(lambda to: signal(barrier, {"sp_0": 0, "sp_1": to}))

    def by_head(t, place):
        loads[t].wait()
        wide[t] = raw[t].astype(jnp.float32).reshape(tokens * HEADS, WIDTH)
        for h in range(HEADS):
            place(h, wide[t, pl.ds(h, tokens, stride=HEADS), :].astype(jnp.bfloat16))

    def place_kv(t):
        def place(h, block):
            stage[h, t] = block

        return place

    def place_q(h, block):
        stage_q[h] = block

    by_head(0, place_kv(0))
    by_head(1, place_kv(1))

    pl.semaphore_wait(barrier, jnp.where(is_owner, head + 1, HEADS))

    @pl.when(is_owner)
    def _():
        mine = ready.at[z - FIRST, x]

        @pl.loop(0, z - FIRST)
        def _(i):
            row = z - 1 - i
            columns_of(lambda to: signal(mine, {"sp_0": row, "sp_1": to}))

        @pl.loop(0, x)
        def _(to):
            signal(mine, {"sp_1": to})

    def kv_copy(row, to):
        h = (row - FIRST) * NX + to
        return pltpu.make_async_remote_copy(
            src_ref=stage.at[h], dst_ref=near.at[me], send_sem=kv_send.at[h], recv_sem=kv_recv.at[me],
            device_id={"sp_0": row, "sp_1": to}, device_id_type=MESH_IDS,
        )

    def q_copy(row, to):
        h = (row - FIRST) * NX + to
        return pltpu.make_async_remote_copy(
            src_ref=stage_q.at[h], dst_ref=queries.at[me], send_sem=q_send.at[h], recv_sem=q_recv.at[me],
            device_id={"sp_0": row, "sp_1": to}, device_id_type=MESH_IDS,
        )

    @pl.loop(FIRST, jnp.minimum(z, FIRST + ROWS))
    def _(row):
        columns_of(lambda to: kv_copy(row, to).start())

    @pl.when(is_owner)
    def _():
        @pl.loop(0, x)
        def _(to):
            kv_copy(z, to).start()

    by_head(2, place_q)

    @pl.when(is_owner)
    def _():
        @pl.loop(x + 1, NX)
        def _(to):
            pl.semaphore_wait(ready.at[z - FIRST, to], 1)
            kv_copy(z, to).start()

    @pl.loop(jnp.maximum(z + 1, FIRST), FIRST + ROWS)
    def _(row):
        def send(to):
            @pl.when(z > 0)
            def _():
                pl.semaphore_wait(ready.at[row - FIRST, to], 1)

            kv_copy(row, to).start()

        columns_of(send)

    @pl.loop(0, ROWS)
    def _(i):
        row = jnp.where(z < NZ // 2, FIRST + ROWS - 1 - i, FIRST + i)

        def send(to):
            @pl.when((row != z) | (to != x))
            def _():
                q_copy(row, to).start()

        columns_of(send)

    columns = pl.ds(pl.multiple_of(jnp.clip(head, 0, HEADS - 1) * WIDTH, WIDTH), WIDTH)

    def back(row, to):
        peer = row * NX + to
        return pltpu.make_async_remote_copy(
            src_ref=outs.at[peer], dst_ref=out_ref.at[:, columns],
            send_sem=back_send.at[peer], recv_sem=back_recv.at[head],
            device_id={"sp_0": row, "sp_1": to}, device_id_type=MESH_IDS,
        )

    def swap(row):
        chunk = pl.ds(row * NX, NX)
        return pltpu.make_async_remote_copy(
            src_ref=near.at[chunk], dst_ref=far.at[chunk],
            send_sem=swap_send.at[row], recv_sem=swap_recv.at[row],
            device_id={"sp_2": 1 - core}, device_id_type=MESH_IDS,
        )

    def of_row(row, body):
        def one(to):
            @pl.when((row != z) | (to != x))
            def _():
                body(row * NX + to)

        columns_of(one)

    def of_row_back(row, act):
        def one(to):
            @pl.when((row != z) | (to != x))
            def _():
                act(back(row, to))

        columns_of(one)

    @pl.when(is_owner)
    def _():
        near[me] = stage[head]
        queries[me] = stage_q[head]
        low = z < NZ // 2

        def nth_row(i):
            own = z + i
            own = jnp.where(own >= jnp.where(low, NZ // 2, NZ), own - NZ // 2, own)
            return jnp.where(i < NZ // 2, own, jnp.where(low, i, NZ - 1 - i))

        @pl.loop(0, NZ)
        def _(i):
            row = nth_row(i)
            of_row(row, lambda s: pltpu.make_async_copy(near.at[s], near.at[s], kv_recv.at[s]).wait())
            swap(row).start()

        @pl.loop(0, NZ)
        def _(row):
            swap(row).wait_recv()

        factor = math.log2(math.e) / WIDTH**0.5
        dims = (((1,), (1,)), ((), ()))

        @pl.loop(0, NZ)
        def _(i):
            row = nth_row(i)
            of_row(row, lambda s: pltpu.make_async_copy(queries.at[s], queries.at[s], q_recv.at[s]).wait())
            q = queries[pl.ds(row * NX, NX)].reshape(NX * tokens, WIDTH)
            k_near = near[:, 0].reshape(CHIPS * tokens, WIDTH)
            k_far = far[:, 0].reshape(CHIPS * tokens, WIDTH)
            s_near = lax.dot_general(q, k_near, dims, preferred_element_type=jnp.float32)
            s_far = lax.dot_general(q, k_far, dims, preferred_element_type=jnp.float32)
            top = jnp.maximum(
                jnp.max(s_near, axis=1, keepdims=True), jnp.max(s_far, axis=1, keepdims=True)
            )
            p_near = jnp.exp2((s_near - top) * factor)
            p_far = jnp.exp2((s_far - top) * factor)
            total = jnp.sum(p_near, axis=1, keepdims=True) + jnp.sum(p_far, axis=1, keepdims=True)
            v_near = near[:, 1].reshape(CHIPS * tokens, WIDTH)
            v_far = far[:, 1].reshape(CHIPS * tokens, WIDTH)
            acc = jnp.dot(p_near.astype(jnp.bfloat16), v_near, preferred_element_type=jnp.float32)
            acc += jnp.dot(p_far.astype(jnp.bfloat16), v_far, preferred_element_type=jnp.float32)
            result = (acc / total).astype(jnp.bfloat16)
            outs[pl.ds(row * NX, NX)] = result.reshape(NX, tokens, WIDTH)
            of_row_back(row, lambda copy: copy.start())

        out_ref[:, columns] = outs[me]

        @pl.loop(0, NZ)
        def _(row):
            swap(row).wait_send()
            of_row_back(row, lambda copy: copy.wait_send())

    @pl.loop(0, HEADS)
    def _(h):
        @pl.when(h != head)
        def _():
            pltpu.make_async_copy(stage.at[h], stage.at[h], kv_send.at[h]).wait()
            pltpu.make_async_copy(stage_q.at[h], stage_q.at[h], q_send.at[h]).wait()
            pltpu.make_async_copy(outs.at[0], outs.at[0], back_recv.at[h]).wait()


def shards(queries, keys, values):
    tokens = queries.shape[0]
    dma = pltpu.SemaphoreType.DMA
    bf16 = jnp.bfloat16
    block = (tokens, WIDTH)
    return pl.pallas_call(
        kernel,
        out_shape=jax.ShapeDtypeStruct((tokens, HEADS * WIDTH), bf16),
        in_specs=[pl.BlockSpec(memory_space=pl.ANY)] * 3,
        out_specs=pl.BlockSpec(memory_space=pltpu.VMEM),
        scratch_shapes=[
            pltpu.VMEM((3, tokens, HEADS, WIDTH), bf16),
            pltpu.VMEM((3, tokens * HEADS, WIDTH), jnp.float32),
            pltpu.VMEM((HEADS, 2, *block), bf16),
            pltpu.VMEM((HEADS, *block), bf16),
            pltpu.VMEM((CHIPS, 2, *block), bf16),
            pltpu.VMEM((CHIPS, *block), bf16),
            pltpu.VMEM((CHIPS, 2, *block), bf16),
            pltpu.VMEM((CHIPS, *block), bf16),
            dma((3,)),
            dma((HEADS,)),
            dma((CHIPS,)),
            dma((HEADS,)),
            dma((CHIPS,)),
            dma((NZ,)),
            dma((NZ,)),
            dma((CHIPS,)),
            dma((HEADS,)),
            pltpu.SemaphoreType.REGULAR((ROWS, NX)),
        ],
        compiler_params=pltpu.CompilerParams(
            collective_id=0, has_side_effects=True, vmem_limit_bytes=54800 * 1024
        ),
    )(queries, keys, values)


def solution(mesh):
    finer = Mesh(mesh.devices.reshape(NZ, NX, 2, mesh.shape["dp"]), ("sp_0", "sp_1", "sp_2", "dp"))
    tokens = P(("dp", "sp_0", "sp_1", "sp_2"), None, None)
    return jax.shard_map(
        shards,
        mesh=finer,
        in_specs=(tokens,) * 3,
        out_specs=P(("dp", "sp_0", "sp_1", "sp_2"), None),
        check_vma=False,
    )
```

time: 76.5 us -> 73.6 us (0.962)
  the two profiles are of different devices: /device:TPU:504 before, /device:TPU:1 now
where the time goes in v2:
time: 73.6 us; the launch traced here: 73.5 us
  Pallas kernels  72.8 us (99%)
    pallas_call x1, Pallas kernels, shards(): pl.pallas_call(kernel, out_shape=jax.ShapeDtypeStruct((tokens, HEADS * WI...  72.8 us

profile of v2, /device:TPU:1, one launch (start us, length us, event | category | flops | bytes accessed | tf_op | source)
XLA Modules:
  0.0 73.5 jit_solution(6278063359447494971)
XLA Ops:
  0.0 72.8 %shard_map.37 = bf16[48,3072]{1,0:T(8,128)(2,1)S(1)} custom-call(bf16[48,24,128]{2,1,0:T(8,128)(2,1)} %q_hbm.1, bf16[48,24,128]{2,1,0:T(8,128)(2,1)} %k_hbm.1, bf16[48,24,128]{2,1,0:T(8,128)(2,1)} %v_hbm.1), custom_call_target="tpu_custom_call" | custom-call | tf_op jit(solution)/shard_map/pallas_call | solution.py:249
  72.8 0.7 copy.5

commit v3 on v2

--- a/solution.py
+++ b/solution.py
@@ -71,9 +71,6 @@
     def place_q(h, block):
         stage_q[h] = block
 
-    by_head(0, place_kv(0))
-    by_head(1, place_kv(1))
-
     pl.semaphore_wait(barrier, jnp.where(is_owner, head + 1, HEADS))
 
     @pl.when(is_owner)
@@ -89,6 +86,9 @@
         def _(to):
             signal(mine, {"sp_1": to})
 
+    by_head(0, place_kv(0))
+    by_head(1, place_kv(1))
+
     def kv_copy(row, to):
         h = (row - FIRST) * NX + to
         return pltpu.make_async_remote_copy(
@@ -103,46 +103,31 @@
             device_id={"sp_0": row, "sp_1": to}, device_id_type=MESH_IDS,
         )
 
-    @pl.loop(FIRST, jnp.minimum(z, FIRST + ROWS))
-    def _(row):
-        columns_of(lambda to: kv_copy(row, to).start())
-
-    @pl.when(is_owner)
-    def _():
-        @pl.loop(0, x)
-        def _(to):
-            kv_copy(z, to).start()
-
     by_head(2, place_q)
 
-    @pl.when(is_owner)
-    def _():
-        @pl.loop(x + 1, NX)
-        def _(to):
-            pl.semaphore_wait(ready.at[z - FIRST, to], 1)
-            kv_copy(z, to).start()
-
-    @pl.loop(jnp.maximum(z + 1, FIRST), FIRST + ROWS)
-    def _(row):
+    def kv_row(row):
         def send(to):
-            @pl.when(z > 0)
+            @pl.when(is_owner & ((row > z) | ((row == z) & (to > x))))
             def _():
                 pl.semaphore_wait(ready.at[row - FIRST, to], 1)
 
-            kv_copy(row, to).start()
+            @pl.when((row != z) | (to != x))
+            def _():
+                kv_copy(row, to).start()
 
         columns_of(send)
 
-    @pl.loop(0, ROWS)
-    def _(i):
-        row = jnp.where(z < NZ // 2, FIRST + ROWS - 1 - i, FIRST + i)
-
+    def q_row(row):
         def send(to):
             @pl.when((row != z) | (to != x))
             def _():
                 q_copy(row, to).start()
 
         columns_of(send)
+
+    for send_row, i in ((kv_row, 0), (kv_row, 1), (kv_row, 2), (q_row, 0), (q_row, 1), (q_row, 2)):
+        send_row(NZ // 2 - 1 - i)
+        send_row(NZ // 2 + i)
 
     columns = pl.ds(pl.multiple_of(jnp.clip(head, 0, HEADS - 1) * WIDTH, WIDTH), WIDTH)
 
@@ -185,9 +170,10 @@
         low = z < NZ // 2
 
         def nth_row(i):
-            own = z + i
+            own = z + i - NZ // 2
             own = jnp.where(own >= jnp.where(low, NZ // 2, NZ), own - NZ // 2, own)
-            return jnp.where(i < NZ // 2, own, jnp.where(low, i, NZ - 1 - i))
+            cross = jnp.where(low, NZ // 2 + i, NZ // 2 - 1 - i)
+            return jnp.where(i < NZ // 2, cross, own)
 
         @pl.loop(0, NZ)
         def _(i):

time: 73.6 us -> 69.1 us (0.939)
  the two profiles are of different devices: /device:TPU:1 before, /device:TPU:504 now
where the time goes in v3:
time: 69.1 us; the launch traced here: 68.9 us
  Pallas kernels  68.2 us (99%)
  local copies, waits for them, and re-layouts  0.72 us (1%)
    pallas_call x1, Pallas kernels, shards(): pl.pallas_call(kernel, out_shape=jax.ShapeDtypeStruct((tokens, HEADS * WI...  68.2 us

profile of v3, /device:TPU:504, one launch (start us, length us, event | category | flops | bytes accessed | tf_op | source)
XLA Modules:
  0.0 68.9 jit_solution(14090254083448881276)
XLA Ops:
  0.0 68.2 %shard_map.37 = bf16[48,3072]{1,0:T(8,128)(2,1)S(1)} custom-call(bf16[48,24,128]{2,1,0:T(8,128)(2,1)} %q_hbm.1, bf16[48,24,128]{2,1,0:T(8,128)(2,1)} %k_hbm.1, bf16[48,24,128]{2,1,0:T(8,128)(2,1)} %v_hbm.1), custom_call_target="tpu_custom_call" | custom-call | tf_op jit(solution)/shard_map/pallas_call | solution.py:235
  68.2 0.7 %copy.5 = bf16[48,3072]{1,0:T(8,128)(2,1)} copy(bf16[48,3072]{1,0:T(8,128)(2,1)S(1)} %shard_map.37) | data formatting | bytes 589824

commit v4 on v3

--- a/solution.py
+++ b/solution.py
@@ -103,8 +103,6 @@
             device_id={"sp_0": row, "sp_1": to}, device_id_type=MESH_IDS,
         )
 
-    by_head(2, place_q)
-
     def kv_row(row):
         def send(to):
             @pl.when(is_owner & ((row > z) | ((row == z) & (to > x))))
@@ -125,9 +123,15 @@
 
         columns_of(send)
 
-    for send_row, i in ((kv_row, 0), (kv_row, 1), (kv_row, 2), (q_row, 0), (q_row, 1), (q_row, 2)):
-        send_row(NZ // 2 - 1 - i)
-        send_row(NZ // 2 + i)
+    for i in range(ROWS // 2):
+        kv_row(NZ // 2 - 1 - i)
+        kv_row(NZ // 2 + i)
+
+    by_head(2, place_q)
+
+    for i in range(ROWS // 2):
+        q_row(NZ // 2 - 1 - i)
+        q_row(NZ // 2 + i)
 
     columns = pl.ds(pl.multiple_of(jnp.clip(head, 0, HEADS - 1) * WIDTH, WIDTH), WIDTH)
 
@@ -181,36 +185,47 @@
             of_row(row, lambda s: pltpu.make_async_copy(near.at[s], near.at[s], kv_recv.at[s]).wait())
             swap(row).start()
 
-        @pl.loop(0, NZ)
-        def _(row):
-            swap(row).wait_recv()
-
         factor = math.log2(math.e) / WIDTH**0.5
         dims = (((1,), (1,)), ((), ()))
 
-        @pl.loop(0, NZ)
-        def _(i):
-            row = nth_row(i)
-            of_row(row, lambda s: pltpu.make_async_copy(queries.at[s], queries.at[s], q_recv.at[s]).wait())
-            q = queries[pl.ds(row * NX, NX)].reshape(NX * tokens, WIDTH)
-            k_near = near[:, 0].reshape(CHIPS * tokens, WIDTH)
-            k_far = far[:, 0].reshape(CHIPS * tokens, WIDTH)
-            s_near = lax.dot_general(q, k_near, dims, preferred_element_type=jnp.float32)
-            s_far = lax.dot_general(q, k_far, dims, preferred_element_type=jnp.float32)
-            top = jnp.maximum(
-                jnp.max(s_near, axis=1, keepdims=True), jnp.max(s_far, axis=1, keepdims=True)
-            )
-            p_near = jnp.exp2((s_near - top) * factor)
-            p_far = jnp.exp2((s_far - top) * factor)
-            total = jnp.sum(p_near, axis=1, keepdims=True) + jnp.sum(p_far, axis=1, keepdims=True)
-            v_near = near[:, 1].reshape(CHIPS * tokens, WIDTH)
-            v_far = far[:, 1].reshape(CHIPS * tokens, WIDTH)
-            acc = jnp.dot(p_near.astype(jnp.bfloat16), v_near, preferred_element_type=jnp.float32)
-            acc += jnp.dot(p_far.astype(jnp.bfloat16), v_far, preferred_element_type=jnp.float32)
+        def attend(i, first=False):
+            own = jnp.where(low, 0, NZ // 2) + 2 * i - NZ // 2
+            cross = jnp.where(low, NZ - 2 - 2 * i, 2 * i)
+            row = jnp.where(i < NZ // 4, cross, own)
+            for r in range(2):
+                of_row(row + r, lambda s: pltpu.make_async_copy(queries.at[s], queries.at[s], q_recv.at[s]).wait())
+            q = queries[pl.ds(row * NX, 2 * NX)].reshape(2 * NX * tokens, WIDTH)
+
+            def half(part):
+                k = part[:, 0].reshape(CHIPS * tokens, WIDTH)
+                v = part[:, 1].reshape(CHIPS * tokens, WIDTH)
+                scores = lax.dot_general(q, k, dims, preferred_element_type=jnp.float32)
+                return scores, v
+
+            scores, v = half(near)
+            top_near = jnp.max(scores, axis=1, keepdims=True)
+            p = jnp.exp2((scores - top_near) * factor)
+            total = jnp.sum(p, axis=1, keepdims=True)
+            acc = jnp.dot(p.astype(jnp.bfloat16), v, preferred_element_type=jnp.float32)
+            if first:
+
+                @pl.loop(0, NZ)
+                def _(row):
+                    swap(row).wait_recv()
+
+            scores, v = half(far)
+            top = jnp.maximum(top_near, jnp.max(scores, axis=1, keepdims=True))
+            p = jnp.exp2((scores - top) * factor)
+            shrink = jnp.exp2((top_near - top) * factor)
+            total = total * shrink + jnp.sum(p, axis=1, keepdims=True)
+            acc = acc * shrink + jnp.dot(p.astype(jnp.bfloat16), v, preferred_element_type=jnp.float32)
             result = (acc / total).astype(jnp.bfloat16)
-            outs[pl.ds(row * NX, NX)] = result.reshape(NX, tokens, WIDTH)
-            of_row_back(row, lambda copy: copy.start())
-
+            outs[pl.ds(row * NX, 2 * NX)] = result.reshape(2 * NX, tokens, WIDTH)
+            for r in range(2):
+                of_row_back(row + r, lambda copy: copy.start())
+
+        attend(0, first=True)
+        pl.loop(1, NZ // 2)(attend)
         out_ref[:, columns] = outs[me]
 
         @pl.loop(0, NZ)

time: 69.1 us -> 66.5 us (0.962)
  Pallas kernels: 68.2 us -> 65.7 us
    pallas_call x1, Pallas kernels: 68.2 us -> 65.7 us  [shards(): pl.pallas_call(kernel, out_shape=jax.ShapeDtypeStruct((tokens, HEADS * WI...]
where the time goes in v4:
time: 66.5 us; the launch traced here: 66.4 us
  Pallas kernels  65.7 us (99%)
  local copies, waits for them, and re-layouts  0.72 us (1%)
    pallas_call x1, Pallas kernels, shards(): pl.pallas_call(kernel, out_shape=jax.ShapeDtypeStruct((tokens, HEADS * WI...  65.7 us

profile of v4, /device:TPU:504, one launch (start us, length us, event | category | flops | bytes accessed | tf_op | source)
XLA Modules:
  0.0 66.4 jit_solution(3248773382407424370)
XLA Ops:
  0.0 65.7 %shard_map.37 = bf16[48,3072]{1,0:T(8,128)(2,1)S(1)} custom-call(bf16[48,24,128]{2,1,0:T(8,128)(2,1)} %q_hbm.1, bf16[48,24,128]{2,1,0:T(8,128)(2,1)} %k_hbm.1, bf16[48,24,128]{2,1,0:T(8,128)(2,1)} %v_hbm.1), custom_call_target="tpu_custom_call" | custom-call | tf_op jit(solution)/shard_map/pallas_call | solution.py:250
  65.7 0.7 %copy.5 = bf16[48,3072]{1,0:T(8,128)(2,1)} copy(bf16[48,3072]{1,0:T(8,128)(2,1)S(1)} %shard_map.37) | data formatting | bytes 589824

commit v5 on v4

--- a/solution.py
+++ b/solution.py
@@ -124,14 +124,15 @@
         columns_of(send)
 
     for i in range(ROWS // 2):
+        kv_row(NZ // 2 + i)
         kv_row(NZ // 2 - 1 - i)
-        kv_row(NZ // 2 + i)
 
     by_head(2, place_q)
 
-    for i in range(ROWS // 2):
-        q_row(NZ // 2 - 1 - i)
-        q_row(NZ // 2 + i)
+    upper = z >= NZ // 2
+    for i in range(ROWS):
+        j = i % (ROWS // 2)
+        q_row(jnp.where(upper == (i < ROWS // 2), NZ // 2 - 1 - j, NZ // 2 + j))
 
     columns = pl.ds(pl.multiple_of(jnp.clip(head, 0, HEADS - 1) * WIDTH, WIDTH), WIDTH)
 

time: 66.5 us -> 65.9 us (level)
  Pallas kernels: 65.7 us -> 65 us
    pallas_call x1, Pallas kernels: 65.7 us -> 65 us  [shards(): pl.pallas_call(kernel, out_shape=jax.ShapeDtypeStruct((tokens, HEADS * WI...]
where the time goes in v5:
time: 65.9 us; the launch traced here: 65.8 us
  Pallas kernels  65 us (99%)
  local copies, waits for them, and re-layouts  0.72 us (1%)
    pallas_call x1, Pallas kernels, shards(): pl.pallas_call(kernel, out_shape=jax.ShapeDtypeStruct((tokens, HEADS * WI...  65 us

profile of v5, /device:TPU:504, one launch (start us, length us, event | category | flops | bytes accessed | tf_op | source)
XLA Modules:
  0.0 65.8 jit_solution(1502919302270162010)
XLA Ops:
  0.0 65.0 %shard_map.37 = bf16[48,3072]{1,0:T(8,128)(2,1)S(1)} custom-call(bf16[48,24,128]{2,1,0:T(8,128)(2,1)} %q_hbm.1, bf16[48,24,128]{2,1,0:T(8,128)(2,1)} %k_hbm.1, bf16[48,24,128]{2,1,0:T(8,128)(2,1)} %v_hbm.1), custom_call_target="tpu_custom_call" | custom-call | tf_op jit(solution)/shard_map/pallas_call | solution.py:251
  65.0 0.7 %copy.5 = bf16[48,3072]{1,0:T(8,128)(2,1)} copy(bf16[48,3072]{1,0:T(8,128)(2,1)S(1)} %shard_map.37) | data formatting | bytes 589824
